TPU v7x, 256 devices: a whole 4x4x8 slice. The times are simulated.
256 devices in a mesh: gx: 32 (over x, y, core), gy: 8 (over z).
Axes of the slice: x: 4, y: 4, z: 8, core: 2. Of those that a mesh axis runs over, the one named last changes fastest.
Arguments:
- points: bfloat16 [524288, 64], P(('gx', 'gy')), may hold values from -6 to 6
- order: int32 [256, 2048], P(('gx', 'gy')), may hold values from 0 to 2047, each once within a row
- probes: bfloat16 [524288, 512], P(('gx', 'gy')), may hold values from -6 to 6
- leaf_basis: bfloat16 [524288, 128], P(('gx', 'gy')), may hold values from -0.125 to 0.125
- leaf_transfer: bfloat16 [256, 128, 128], P(('gx', 'gy')), may hold values from -0.4375 to 0.4375
- fine_transfer: bfloat16 [32, 6, 128, 128], P('gx'), may hold values from -0.4375 to 0.4375
- coarse_transfer: bfloat16 [60, 128, 128], replicated, may hold values from -0.4375 to 0.4375
- fine_couple: bfloat16 [32, 7, 2, 128, 128], P('gx'), may hold values from -0.5 to 0.5
- coarse_couple: bfloat16 [31, 2, 128, 128], replicated, may hold values from -0.5 to 0.5
Outputs:
- kernel_product: bfloat16 [524288, 512], P(('gx', 'gy'))
- derivative_product: bfloat16 [524288, 512], P(('gx', 'gy'))
Inputs may be any that keep to these rules, and one draw needn't show every extreme that they name: `order`: each row holds every number from 0 to 2047 once.
All inputs are finite; a program needn't handle non-finite values.
Results may differ from a plain program's by a relative error of at most 0.0049.
Values sent between devices are 32-bit elements; how exact they have to be, the bound alone decides.
No kernel may reach another device: no remote copies, remote signals or barrier semaphores. Data moves between devices by JAX's collectives and lax.ppermute only.
A program may use at most 128 MiB of HBM per device.

v0:
```python
import functools
import math

import jax
import jax.numpy as jnp
from jax import lax
from jax.experimental import pallas as pl
from jax.experimental.pallas import tpu as pltpu
from jax.sharding import PartitionSpec as P


length_scale = 3.25
bf16 = jnp.bfloat16
f32 = jnp.float32
MIB = 1 << 20


def vmem(count):
    return [pl.BlockSpec(memory_space=pltpu.VMEM)] * count


def held_in_hbm(*arrays):
    return [pltpu.with_memory_space_constraint(array, pltpu.HBM) for array in arrays]


def hbm(count):
    return [pl.BlockSpec(memory_space=pltpu.HBM)] * count


def smem():
    return pl.BlockSpec(memory_space=pltpu.SMEM)


def params(mib):
    return pltpu.CompilerParams(vmem_limit_bytes=mib * MIB)


def cost(flops, moved):
    return pl.CostEstimate(flops=int(flops), bytes_accessed=int(moved), transcendentals=0)


def dot_nn(a, b):
    return lax.dot_general(a, b, (((1,), (0,)), ((), ())), preferred_element_type=f32)


def dot_nt(a, b):
    return lax.dot_general(a, b, (((1,), (1,)), ((), ())), preferred_element_type=f32)


def split(x):
    high = x.astype(bf16)
    low = (x - high.astype(f32)).astype(bf16)
    return jnp.concatenate([high, low], axis=0)


def exact(dot, x, w):
    rows = x.shape[0]
    both = dot(split(x), w)
    return both[:rows] + both[rows:]


def order_columns(order_ref, start, rows):
    pieces = []
    for piece in range(rows // 128):
        line = order_ref[0:1, pl.ds(start + piece * 128, 128)]
        pieces.append(jnp.transpose(jnp.broadcast_to(line, (128, 128))))
    return jnp.concatenate(pieces, axis=0).astype(jnp.int16)


def one_hot(columns, start, width):
    lane = lax.broadcasted_iota(jnp.int32, columns.shape, 1)
    tiles = []
    for tile in range(width // 128):
        lanes = (lane + (start + tile * 128)).astype(jnp.int16)
        tiles.append(jnp.where(columns == lanes, bf16(1.0), bf16(0.0)))
    return jnp.concatenate(tiles, axis=1)


def leaf_up_kernel(
    order_hbm,
    basis_hbm,
    probes_hbm,
    transfer_hbm,
    h_ref,
    lift_ref,
    order_ref,
    basis_ref,
    probes_ref,
    transfer_ref,
    columns_ref,
    hot_ref,
    stored_ref,
    sems,
):
    copies = [
        pltpu.make_async_copy(source, target, sems.at[n])
        for n, (source, target) in enumerate(
            (
                (order_hbm, order_ref),
                (basis_hbm, basis_ref),
                (probes_hbm, probes_ref),
                (transfer_hbm, transfer_ref),
            )
        )
    ]
    for copy in copies:
        copy.start()
    leaf = basis_ref.shape[0]
    step = 512
    copies[0].wait()
    columns_ref[...] = order_columns(order_ref, 0, leaf)
    copies[1].wait()
    basis_t = jnp.transpose(basis_ref[...])
    for start in range(0, leaf, step):
        hot_ref[:, pl.ds(start, step)] = one_hot(columns_ref[...], start, step)
        stored_ref[:, pl.ds(start, step)] = dot_nn(basis_t, hot_ref[:, pl.ds(start, step)]).astype(bf16)
    copies[2].wait()
    h_t = jnp.transpose(dot_nn(stored_ref[...], probes_ref[...]))
    copies[3].wait()
    h_ref[...] = h_t
    lift_ref[...] = exact(dot_nn, h_t, transfer_ref[0])


def leaf_up(order, basis, probes, transfer):
    leaf, rank = basis.shape
    columns = probes.shape[1]
    shape = jax.ShapeDtypeStruct((columns, rank), f32)
    return pl.pallas_call(
        leaf_up_kernel,
        out_shape=(shape, shape),
        in_specs=hbm(4),
        out_specs=tuple(vmem(2)),
        scratch_shapes=[
            pltpu.VMEM(order.shape, order.dtype),
            pltpu.VMEM(basis.shape, bf16),
            pltpu.VMEM(probes.shape, bf16),
            pltpu.VMEM(transfer.shape, bf16),
            pltpu.VMEM((leaf, 128), jnp.int16),
            pltpu.VMEM((leaf, leaf), bf16),
            pltpu.VMEM((rank, leaf), bf16),
            pltpu.SemaphoreType.DMA((4,)),
        ],
        compiler_params=params(24),
        cost_estimate=cost(4e9, 3 * MIB),
        name="leaf_up",
    )(*held_in_hbm(order, basis, probes, transfer))


def near_kernel(order_ref, points_ref, transfer_ref, basis_ref, probes_hbm, *refs, first):
    extra = refs[:3] if len(refs) > 10 else None
    outs, (right_ref, left_ref, hot_ref, both_ref, probes_ref, sem) = refs[:-6], refs[-6:]
    kernel_ref, derivative_ref, wide_ref = outs[len(outs) - 3 :] if extra is None else outs[3:6]
    features, leaf = points_ref.shape
    rows = kernel_ref.shape[0]
    step = 256
    slope = math.sqrt(3.0) / length_scale
    rate = -slope * math.log2(math.e)
    block = pl.program_id(0)
    copy = pltpu.make_async_copy(probes_hbm, probes_ref, sem)

    @pl.when(block == 0)
    def _():
        copy.start()
        values = points_ref[...].astype(f32)
        norm = jnp.sum(values * values, axis=0, keepdims=True)
        high = norm.astype(bf16).astype(f32)
        rest = norm - high
        middle = rest.astype(bf16).astype(f32)
        low = rest - middle
        line = lax.broadcasted_iota(jnp.int32, (128 - features, leaf), 0)

        def tail(norm_line, ones_line):
            ones = (line >= ones_line) & (line < ones_line + 3)
            out = jnp.where(ones, 1.0, 0.0)
            for offset, piece in enumerate((high, middle, low)):
                out = jnp.where(line == norm_line + offset, piece, out)
            return out

        right_ref[...] = jnp.concatenate([values, tail(0, 3)], axis=0).astype(bf16)
        left_ref[...] = jnp.concatenate([-2.0 * values, tail(3, 0)], axis=0).astype(bf16)
        if extra is not None:
            place_ref, sibling_ref, couple_ref = extra
            place = place_ref[1]
            size = sibling_ref.shape[0]
            g = coupled(sibling_ref[...], couple_ref.at[0], place >> 1, place & 1).astype(bf16)
            outs[6][0] = g[:size]
            outs[6][1] = g[size:]

    columns = order_columns(order_ref, first + block * rows, rows)
    hot_ref[...] = one_hot(columns, 0, leaf)
    rows_left = dot_nt(hot_ref[...], left_ref[...]).astype(bf16)
    basis = basis_ref[...]
    rank = basis.shape[1]
    wide_ref[:, :rank] = dot_nn(basis, transfer_ref[0]).astype(bf16)
    wide_ref[:, rank:] = basis
    for start in range(0, leaf, step):
        squared = dot_nn(rows_left, right_ref[:, pl.ds(start, step)])
        squared = jnp.maximum(squared, 1e-30)
        root = squared * lax.rsqrt(squared)
        falloff = jnp.exp2(root * rate)
        both_ref[0:rows, pl.ds(start, step)] = ((1.0 + root * slope) * falloff).astype(bf16)
        both_ref[rows : 2 * rows, pl.ds(start, step)] = (squared * falloff).astype(bf16)

    @pl.when(block == 0)
    def _():
        copy.wait()

    sums = dot_nn(both_ref[...], probes_ref[...])
    kernel_ref[...] = sums[:rows].astype(bf16)
    derivative_ref[...] = (sums[rows:] * (slope * slope)).astype(bf16)


def near_part(order, points, transfer, basis, probes, extra, first, count, rows):
    leaf, columns = probes.shape
    rank = basis.shape[1]
    held = first // rows
    out_shape = [pltpu.HBM((count * rows, width), bf16) for width in (columns, columns, 2 * rank)]
    out_specs = [pl.BlockSpec((rows, width), lambda i: (i, 0)) for width in (columns, columns, 2 * rank)]
    extra_specs = []
    if extra:
        out_shape.append(pltpu.HBM((2, columns, rank), bf16))
        out_specs.append(pl.BlockSpec((2, columns, rank), lambda i: (0, 0, 0)))
        extra_specs = [smem()] + [
            pl.BlockSpec(array.shape, functools.partial(lambda n, i: (0,) * n, array.ndim)) for array in extra[1:]
        ]
    whole = lambda i: (0, 0)
    return pl.pallas_call(
        functools.partial(near_kernel, first=first),
        grid=(count,),
        out_shape=tuple(out_shape),
        in_specs=[
            pl.BlockSpec(order.shape, whole),
            pl.BlockSpec(points.shape, whole),
            pl.BlockSpec(transfer.shape, lambda i: (0, 0, 0)),
            pl.BlockSpec((rows, rank), lambda i: (held + i, 0)),
            pl.BlockSpec(memory_space=pltpu.HBM),
        ]
        + extra_specs,
        out_specs=tuple(out_specs),
        scratch_shapes=[
            pltpu.VMEM((128, leaf), bf16),
            pltpu.VMEM((128, leaf), bf16),
            pltpu.VMEM((rows, leaf), bf16),
            pltpu.VMEM((2 * rows, leaf), bf16),
            pltpu.VMEM(probes.shape, bf16),
            pltpu.SemaphoreType.DMA,
        ],
        compiler_params=params(32),
        cost_estimate=cost(2.0 * count * rows * leaf * (columns * 2 + 512), 6 * MIB),
    )(order, points, transfer, *held_in_hbm(basis, probes), *extra)


def fine_up_kernel(lift_ref, transfer_ref, one_ref, two_ref, three_ref):
    twos = []
    for node in range(2):
        total = None
        for child in (2 * node, 2 * node + 1):
            value = lift_ref[2 * child] + lift_ref[2 * child + 1]
            one_ref[child] = value
            moved = exact(dot_nn, value, transfer_ref[0, child])
            total = moved if total is None else total + moved
        two_ref[node] = total
        twos.append(total)
    three_ref[...] = exact(dot_nn, twos[0], transfer_ref[0, 4]) + exact(dot_nn, twos[1], transfer_ref[0, 5])


def fine_up(lifts, transfer):
    columns, rank = lifts.shape[1:]
    return pl.pallas_call(
        fine_up_kernel,
        out_shape=(
            jax.ShapeDtypeStruct((4, columns, rank), f32),
            jax.ShapeDtypeStruct((2, columns, rank), f32),
            jax.ShapeDtypeStruct((columns, rank), f32),
        ),
        in_specs=vmem(2),
        out_specs=tuple(vmem(3)),
        compiler_params=params(8),
        cost_estimate=cost(1e9, MIB),
        name="fine_up",
    )(lifts, transfer)


def pair_up_kernel(place_ref, own_ref, other_ref, transfer_ref, out_ref):
    place = place_ref[0]
    out_ref[...] = exact(dot_nn, own_ref[...], transfer_ref[place]) + exact(
        dot_nn, other_ref[...], transfer_ref[place ^ 1]
    )


def pair_up(place, own, other, transfer):
    return pl.pallas_call(
        pair_up_kernel,
        out_shape=jax.ShapeDtypeStruct(own.shape, f32),
        in_specs=[smem()] + vmem(3),
        out_specs=vmem(1)[0],
        compiler_params=params(8),
        cost_estimate=cost(1e8, MIB // 8),
        name="pair_up",
    )(place, own, other, transfer)


def quad_up_kernel(place_ref, own_ref, x1_ref, x2_ref, x3_ref, transfer_ref, pair_ref, top_ref):
    place = place_ref[0] >> 1
    base = 32
    values = (own_ref, x1_ref, x2_ref, x3_ref)
    moved = [exact(dot_nn, value[...], transfer_ref[base + (place ^ flip)]) for flip, value in enumerate(values)]
    mine = moved[0] + moved[1]
    theirs = moved[2] + moved[3]
    pair_ref[...] = theirs
    place = place >> 1
    base = 48
    top_ref[...] = exact(dot_nn, mine, transfer_ref[base + place]) + exact(
        dot_nn, theirs, transfer_ref[base + (place ^ 1)]
    )


def quad_up(place, own, x1, x2, x3, transfer):
    shape = jax.ShapeDtypeStruct(own.shape, f32)
    return pl.pallas_call(
        quad_up_kernel,
        out_shape=(shape, shape),
        in_specs=[smem()] + vmem(5),
        out_specs=tuple(vmem(2)),
        compiler_params=params(8),
        cost_estimate=cost(1e8, MIB // 8),
        name="quad_up",
    )(place, own, x1, x2, x3, transfer)


def coupled(value, pair_ref, index, side):
    rank = value.shape[1]
    sides = []
    for k in range(2):
        matrix = pair_ref[index, k].astype(f32)
        sides.append(jnp.where(side == 0, jnp.transpose(matrix), matrix).astype(bf16))
    both = exact(dot_nn, value, jnp.concatenate(sides, axis=1))
    return jnp.concatenate([both[:, :rank], both[:, rank:]], axis=0)


def turn_kernel(
    place_ref,
    top_ref,
    x1_ref,
    x2_ref,
    x3_ref,
    five_ref,
    four_ref,
    three_ref,
    two_ref,
    one_ref,
    coarse_ref,
    couple_ref,
    fine_ref,
    fine_couple_ref,
    out_ref,
):
    place = place_ref[0]
    at = place >> 3
    far = exact(dot_nn, x2_ref[...], coarse_ref[56 + (at ^ 2)]) + exact(
        dot_nn, x3_ref[...], coarse_ref[56 + (at ^ 3)]
    )
    z = coupled(far, couple_ref, 30, at >> 1)
    levels = (
        (x1_ref, 28, 56, 3),
        (five_ref, 24, 48, 2),
        (four_ref, 16, 32, 1),
        (three_ref, 0, 0, 0),
    )
    for sibling_ref, couple_base, base, shift in levels:
        at = place >> shift
        g = coupled(sibling_ref[...], couple_ref, couple_base + (at >> 1), at & 1)
        z = g + exact(dot_nt, z, coarse_ref[base + at])
    for node in range(2):
        g = coupled(two_ref[1 - node], fine_couple_ref.at[0], 6, node)
        z_two = g + exact(dot_nt, z, fine_ref[0, 4 + node])
        for child in (2 * node, 2 * node + 1):
            g = coupled(one_ref[child ^ 1], fine_couple_ref.at[0], 4 + node, child & 1)
            z_one = g + exact(dot_nt, z_two, fine_ref[0, child])
            out_ref[2 * child] = z_one
            out_ref[2 * child + 1] = z_one


def turn(place, *operands):
    columns, rank = operands[0].shape
    return pl.pallas_call(
        turn_kernel,
        out_shape=jax.ShapeDtypeStruct((8, 2 * columns, rank), f32),
        in_specs=[smem()] + vmem(len(operands)),
        out_specs=vmem(1)[0],
        compiler_params=params(16),
        cost_estimate=cost(1e9, MIB),
        name="turn",
    )(place, *operands)


def finish_kernel(down_ref, couple_hbm, *refs):
    parts_hbm = refs[:6]
    out_k_hbm, out_d_hbm, couple_ref, wide_ref, near_ref, held_ref, in_sems, out_sems = refs[6:]
    part = down_ref.shape[1] // 2
    arrivals = [pltpu.make_async_copy(couple_hbm, couple_ref, in_sems.at[0])]
    spans = []
    start = 0
    for half in range(2):
        near_k, near_d, wide = parts_hbm[3 * half : 3 * half + 3]
        span = pl.ds(start, near_k.shape[0])
        spans.append(span)
        start += near_k.shape[0]
        for source, target in (
            (wide, wide_ref.at[span, :]),
            (near_k, near_ref.at[0, span, :]),
            (near_d, near_ref.at[1, span, :]),
        ):
            arrivals.append(pltpu.make_async_copy(source, target, in_sems.at[len(arrivals)]))
    for copy in arrivals:
        copy.start()
    parents = [
        jnp.concatenate([down_ref[s, k * part : (k + 1) * part].astype(bf16) for s in range(down_ref.shape[0])], axis=0)
        for k in range(2)
    ]
    arrivals[0].wait()
    both = [jnp.concatenate([parents[k], couple_ref[k]], axis=1) for k in range(2)]
    departures = []
    for half, span in enumerate(spans):
        arrivals[1 + 3 * half].wait()
        for k, out_hbm in enumerate((out_k_hbm, out_d_hbm)):
            arrivals[2 + 3 * half + k].wait()
            far = dot_nt(wide_ref[span, :], both[k])
            held_ref[k, span, :] = (near_ref[k, span, :].astype(f32) + far).astype(bf16)
            departures.append(
                pltpu.make_async_copy(held_ref.at[k, span, :], out_hbm.at[span, :], out_sems.at[len(departures)])
            )
            departures[-1].start()
    for copy in departures:
        copy.wait()


def finish(down, couple, *parts):
    leaf = parts[0].shape[0] + parts[3].shape[0]
    columns = parts[0].shape[1]
    wide = parts[2].shape[1]
    shape = jax.ShapeDtypeStruct((leaf, columns), bf16)
    return pl.pallas_call(
        finish_kernel,
        out_shape=(shape, shape),
        in_specs=vmem(1) + hbm(1 + len(parts)),
        out_specs=tuple(hbm(2)),
        scratch_shapes=[
            pltpu.VMEM(couple.shape, bf16),
            pltpu.VMEM((leaf, wide), bf16),
            pltpu.VMEM((2, leaf, columns), bf16),
            pltpu.VMEM((2, leaf, columns), bf16),
            pltpu.SemaphoreType.DMA((7,)),
            pltpu.SemaphoreType.DMA((4,)),
        ],
        compiler_params=params(24),
        cost_estimate=cost(1e9, 10 * MIB),
        name="finish",
    )(down, *held_in_hbm(couple, *parts))


def swap(x, axis, mask):
    return lax.ppermute(x, axis, [(i, i ^ mask) for i in range(lax.axis_size(axis))])


def per_device(
    points, order, probes, leaf_basis, leaf_transfer, fine_transfer, coarse_transfer, fine_couple, coarse_couple
):
    group = lax.axis_size("gy")
    place = jnp.stack([lax.axis_index("gx"), lax.axis_index("gy")]).astype(jnp.int32)
    points_t = jnp.transpose(points)
    h_t, lift_t = leaf_up(order, leaf_basis, probes, leaf_transfer)
    columns, rank = h_t.shape
    leaf = probes.shape[0]
    order_a, lift_t = lax.optimization_barrier((order, lift_t))
    lifts = lax.all_to_all(lift_t.reshape(group, columns // group, rank), "gy", 0, 0)
    rows = leaf // 4
    near_a = near_part(order_a, points_t, leaf_transfer, leaf_basis, probes, (), 0, 2, rows)
    near_a, lifts = lax.optimization_barrier((near_a, lifts))
    one, two, three = fine_up(lifts, fine_transfer)
    three_sibling = swap(three, "gx", 1)
    four = pair_up(place, three, three_sibling, coarse_transfer)
    four, h_t = lax.optimization_barrier((four, h_t))
    y1, y2, y3 = [swap(four, "gx", mask << 1) for mask in (1, 2, 3)]
    leaf_sibling = swap(h_t, "gy", 1)
    five_sibling, six = quad_up(place, four, y1, y2, y3, coarse_transfer)
    x1, x2, x3 = [swap(six, "gx", mask << 3) for mask in (1, 2, 3)]
    sent = turn(
        place,
        six,
        x1,
        x2,
        x3,
        five_sibling,
        y1,
        three_sibling,
        two,
        one,
        coarse_transfer,
        coarse_couple,
        fine_transfer,
        fine_couple,
    )
    order_b, leaf_sibling, sent = lax.optimization_barrier((order, leaf_sibling, sent))
    down = lax.all_to_all(sent, "gy", 0, 0)
    extra = (place, leaf_sibling, fine_couple)
    near_b = near_part(order_b, points_t, leaf_transfer, leaf_basis, probes, extra, 2 * rows, 2, rows)
    return finish(down, near_b[3], *near_a, *near_b[:3])


def solution(mesh):
    placed = (
        P(("gx", "gy"), None),
        P(("gx", "gy"), None),
        P(("gx", "gy"), None),
        P(("gx", "gy"), None),
        P(("gx", "gy"), None, None),
        P("gx", None, None, None),
        P(),
        P("gx", None, None, None, None),
        P(),
    )
    return jax.shard_map(
        per_device,
        mesh=mesh,
        in_specs=placed,
        out_specs=(P(("gx", "gy"), None), P(("gx", "gy"), None)),
        check_vma=False,
    )
```

profile of v0, /device:TPU:16, one launch (start us, length us, event | category | flops | bytes accessed | tf_op | source)
XLA Modules:
  0.0 74.3 jit_solution(195641542681095692)
XLA Ops:
  0.6 0.0 copy-start.5
  0.6 0.0 copy-start.6
  0.6 0.0 copy-start.4
  0.7 4.3 %leaf_up.1 = (f32[512,128]{1,0:T(8,128)S(1)}, f32[512,128]{1,0:T(8,128)}) custom-call(s32[1,2048]{1,0:T(1,128)} %order_ref.1, bf16[2048,128]{1,0:T(8,128)(2,1)} %basis_ref.3, bf16[2048,512]{1,0:T(8,128)(2,1)} %probes_hbm.5, bf16[1,128,128]{2,1,0:T(8,128)(2,1)} %transfer_ref.9), custom_call_target="tpu_custom_call" | custom-call | flops 4000000000 | bytes 3145728 | tf_op jit(solution)/shard_map/leaf_up/pallas_call | solution.py:128
  5.0 8.5 %all-to-all-start = ((f32[8,64,128]{2,1,0:T(8,128)}), f32[8,64,128]{2,1,0:T(8,128)S(1)}, u32[]{:S(2)}, u32[]{:S(2)}) async-start(f32[8,64,128]{2,1,0:T(8,128)} %bitcast.3), calls=%async_computation | async-start | bytes 524288 | tf_op jit(solution)/shard_map/all_to_all | solution.py:476
  13.5 0.0 copy-done.5
  13.5 0.0 copy-done.6
  13.5 0.0 copy-done.4
  13.5 0.0 copy-start.3
  13.5 12.2 %shard_map.104 = (bf16[1024,512]{1,0:T(8,128)(2,1)}, bf16[1024,512]{1,0:T(8,128)(2,1)}, bf16[1024,256]{1,0:T(8,128)(2,1)}) custom-call(s32[1,2048]{1,0:T(1,128)S(1)} %copy-done.6, bf16[64,2048]{1,0:T(8,128)(2,1)S(1)} %bitcast.4, bf16[1,128,128]{2,1,0:T(8,128)(2,1)S(1)} %copy-done.5, bf16[2048,128]{1,0:T(8,128)(2,1)} %basis_ref.3, bf16[2048,512]{1,0:T(8,128)(2,1)} %probes_hbm.5), custom_call_target="tpu_custom_call" | custom-call | flops 6442450944 | bytes 6291456 | tf_op jit(solution)/shard_map/pallas_call | solution.py:227
  25.7 0.0 copy-start
  25.8 0.0 all-to-all-done.lift_ref
  25.8 0.0 copy-done.3
  25.8 0.3 fine_up.1
  26.1 0.0 copy-start.1
  26.1 0.0 copy-start.2
  26.1 0.1 collective-permute-start
  26.2 0.1 pad_add_fusion.place_ref.refs_0_
  26.3 1.1 %collective-permute-done.other_ref.three_ref = f32[64,128]{1,0:T(8,128)S(1)} collective-permute-done((f32[64,128]{1,0:T(8,128)S(1)}, f32[64,128]{1,0:T(8,128)S(1)}, u32[]{:S(2)}, u32[]{:S(2)}) %collective-permute-start) | collective-permute-done | bytes 32800 | tf_op jit(solution)/shard_map/ppermute | solution.py:463
  27.4 0.0 copy-done
  27.4 0.7 pair_up.1.own_ref
  28.1 2.1 %collective-permute-start.1 = (f32[512,128]{1,0:T(8,128)S(1)}, f32[512,128]{1,0:T(8,128)S(1)}, u32[]{:S(2)}, u32[]{:S(2)}) collective-permute-start(f32[512,128]{1,0:T(8,128)S(1)} %get-tuple-element.36), channel_id=1, source_target_pairs={{0,1},{1,0},{2,3},{3,2},{4,5},{5,4},{6,7},{7,6},{8,9},{9,8},{10,11... | collective-permute-start | bytes 786440 | tf_op jit(solution)/shard_map/ppermute | solution.py:463
  30.2 0.4 collective-permute-start.4
  30.6 2.9 %collective-permute-start.3 = (f32[64,128]{1,0:T(8,128)S(1)}, f32[64,128]{1,0:T(8,128)S(1)}, u32[]{:S(2)}, u32[]{:S(2)}) collective-permute-start(f32[64,128]{1,0:T(8,128)S(1)} %pair_up.1.own_ref), channel_id=1, source_target_pairs={{0,32},{8,40},{16,48},{24,56},{32,0},{40,8},{48,16},{56,24},{64,96... | collective-permute-start | bytes 98312 | tf_op jit(solution)/shard_map/ppermute | solution.py:463
  33.5 0.7 %collective-permute-start.2 = (f32[64,128]{1,0:T(8,128)S(1)}, f32[64,128]{1,0:T(8,128)S(1)}, u32[]{:S(2)}, u32[]{:S(2)}) collective-permute-start(f32[64,128]{1,0:T(8,128)S(1)} %pair_up.1.own_ref), channel_id=1, source_target_pairs={{0,16},{8,24},{16,0},{24,8},{32,48},{40,56},{48,32},{56,40},{64,80... | collective-permute-start | bytes 98312 | tf_op jit(solution)/shard_map/ppermute | solution.py:463
  34.3 0.0 collective-permute-done.4.x3_ref
  34.3 1.8 %collective-permute-done.3.x2_ref = f32[64,128]{1,0:T(8,128)S(1)} collective-permute-done((f32[64,128]{1,0:T(8,128)S(1)}, f32[64,128]{1,0:T(8,128)S(1)}, u32[]{:S(2)}, u32[]{:S(2)}) %collective-permute-start.3) | collective-permute-done | bytes 32800 | tf_op jit(solution)/shard_map/ppermute | solution.py:463
  36.0 1.4 %collective-permute-done.2.x1_ref.four_ref = f32[64,128]{1,0:T(8,128)S(1)} collective-permute-done((f32[64,128]{1,0:T(8,128)S(1)}, f32[64,128]{1,0:T(8,128)S(1)}, u32[]{:S(2)}, u32[]{:S(2)}) %collective-permute-start.2) | collective-permute-done | bytes 32800 | tf_op jit(solution)/shard_map/ppermute | solution.py:463
  37.4 0.9 %quad_up.1 = (f32[64,128]{1,0:T(8,128)S(1)}, f32[64,128]{1,0:T(8,128)S(1)}) custom-call(s32[2]{0:T(128)S(1)} %pad_add_fusion.place_ref.refs_0_, f32[64,128]{1,0:T(8,128)S(1)} %pair_up.1.own_ref, f32[64,128]{1,0:T(8,128)S(1)} %collective-permute-done.2.x1_ref.four_ref, f32[64,128]{1,0:T(8,128)S(1)} %collective-permute-done.3.x2_ref, ...), custom_call_target="tpu_custom_call" | custom-call | flops 100000000 | bytes 131072 | tf_op jit(solution)/shard_map/quad_up/pallas_call | solution.py:320
  38.3 2.8 %collective-permute-start.7 = (f32[64,128]{1,0:T(8,128)S(1)}, f32[64,128]{1,0:T(8,128)S(1)}, u32[]{:S(2)}, u32[]{:S(2)}) collective-permute-start(f32[64,128]{1,0:T(8,128)S(1)} %get-tuple-element.38.top_ref), channel_id=1, source_target_pairs={{0,192},{8,200},{16,208},{24,216},{32,224},{40,232},{48,240},{56,2... | collective-permute-start | bytes 98312 | tf_op jit(solution)/shard_map/ppermute | solution.py:463
  41.1 0.8 %collective-permute-start.6 = (f32[64,128]{1,0:T(8,128)S(1)}, f32[64,128]{1,0:T(8,128)S(1)}, u32[]{:S(2)}, u32[]{:S(2)}) collective-permute-start(f32[64,128]{1,0:T(8,128)S(1)} %get-tuple-element.38.top_ref), channel_id=1, source_target_pairs={{0,128},{8,136},{16,144},{24,152},{32,160},{40,168},{48,176},{56,1... | collective-permute-start | bytes 98312 | tf_op jit(solution)/shard_map/ppermute | solution.py:463
  41.9 0.5 collective-permute-start.5
  42.4 1.0 %collective-permute-done.7.x3_ref = f32[64,128]{1,0:T(8,128)S(1)} collective-permute-done((f32[64,128]{1,0:T(8,128)S(1)}, f32[64,128]{1,0:T(8,128)S(1)}, u32[]{:S(2)}, u32[]{:S(2)}) %collective-permute-start.7) | collective-permute-done | bytes 32800 | tf_op jit(solution)/shard_map/ppermute | solution.py:463
  43.4 3.0 %collective-permute-done.6.x2_ref = f32[64,128]{1,0:T(8,128)S(1)} collective-permute-done((f32[64,128]{1,0:T(8,128)S(1)}, f32[64,128]{1,0:T(8,128)S(1)}, u32[]{:S(2)}, u32[]{:S(2)}) %collective-permute-start.6) | collective-permute-done | bytes 32800 | tf_op jit(solution)/shard_map/ppermute | solution.py:463
  46.5 0.0 collective-permute-done.5.x1_ref
  46.5 0.0 copy-done.1
  46.5 0.0 copy-done.2
  46.5 2.7 %turn.1 = f32[8,128,128]{2,1,0:T(8,128)} custom-call(s32[2]{0:T(128)S(1)} %pad_add_fusion.place_ref.refs_0_, f32[64,128]{1,0:T(8,128)S(1)} %get-tuple-element.38.top_ref, f32[64,128]{1,0:T(8,128)S(1)} %collective-permute-done.5.x1_ref, f32[64,128]{1,0:T(8,128)S(1)} %collective-permute-done.6.x2_ref, f32[64,128]{1,0:T(8,128)S(1)} %collective-permute-done.7.x3_ref, ...), custom_call_target="tpu_custom_call" | custom-call | flops 1000000000 | bytes 1048576 | tf_op jit(solution)/shard_map/turn/pallas_call | solution.py:386
  49.2 0.0 collective-permute-done.1.refs_1_
  49.2 5.7 %all-to-all-start.1 = ((f32[8,128,128]{2,1,0:T(8,128)}), f32[8,128,128]{2,1,0:T(8,128)S(1)}, u32[]{:S(2)}, u32[]{:S(2)}) async-start(f32[8,128,128]{2,1,0:T(8,128)} %turn.1), calls=%async_computation.1 | async-start | bytes 1048576 | tf_op jit(solution)/shard_map/all_to_all | solution.py:505
  55.0 12.5 %shard_map.105 = (bf16[1024,512]{1,0:T(8,128)(2,1)}, bf16[1024,512]{1,0:T(8,128)(2,1)}, bf16[1024,256]{1,0:T(8,128)(2,1)}, bf16[2,512,128]{2,1,0:T(8,128)(2,1)}) custom-call(s32[1,2048]{1,0:T(1,128)S(1)} %copy-done.6, bf16[64,2048]{1,0:T(8,128)(2,1)S(1)} %bitcast.5, bf16[1,128,128]{2,1,0:T(8,128)(2,1)S(1)} %copy-done.5, bf16[2048,128]{1,0:T(8,128)(2,1)} %basis_ref.3, ...), custom_call_target="tpu_custom_call" | custom-call | flops 6442450944 | bytes 6291456 | tf_op jit(solution)/shard_map/pallas_call | solution.py:227
  67.4 2.3 %all-to-all-done.1.down_ref = f32[8,128,128]{2,1,0:T(8,128)S(1)} async-done(((f32[8,128,128]{2,1,0:T(8,128)}), f32[8,128,128]{2,1,0:T(8,128)S(1)}, u32[]{:S(2)}, u32[]{:S(2)}) %all-to-all-start.1) | async-done | bytes 524320 | tf_op jit(solution)/shard_map/all_to_all | solution.py:505
  69.7 4.4 %finish.1 = (bf16[2048,512]{1,0:T(8,128)(2,1)}, bf16[2048,512]{1,0:T(8,128)(2,1)}) custom-call(f32[8,128,128]{2,1,0:T(8,128)S(1)} %all-to-all-done.1.down_ref, bf16[2,512,128]{2,1,0:T(8,128)(2,1)} %get-tuple-element.45.couple_hbm, bf16[1024,512]{1,0:T(8,128)(2,1)} %get-tuple-element.46.refs_0_, bf16[1024,512]{1,0:T(8,128)(2,1)} %get-tuple-element.47.refs_1_, ...), custom_call_target="tpu_custom_call" | custom-call | flops 1000000000 | bytes 10485760 | tf_op jit(solution)/shard_map/finish/pallas_call | solution.py:443
Async XLA Ops:
  0.6 12.8 %copy-start.5 = (bf16[1,128,128]{2,1,0:T(8,128)(2,1)S(1)}, bf16[1,128,128]{2,1,0:T(8,128)(2,1)}, u32[]{:S(2)}) copy-start(bf16[1,128,128]{2,1,0:T(8,128)(2,1)} %transfer_ref.9) | copy-start | bytes 98308
  0.6 12.8 %copy-start.6 = (s32[1,2048]{1,0:T(1,128)S(1)}, s32[1,2048]{1,0:T(1,128)}, u32[]{:S(2)}) copy-start(s32[1,2048]{1,0:T(1,128)} %order_ref.1) | copy-start | bytes 24580
  0.6 12.8 %copy-start.4 = (bf16[2048,64]{0,1:T(8,128)(2,1)S(1)}, bf16[2048,64]{0,1:T(8,128)(2,1)}, u32[]{:S(2)}) copy-start(bf16[2048,64]{0,1:T(8,128)(2,1)} %param.9) | copy-start | bytes 786436
  5.0 20.8 %all-to-all-start = ((f32[8,64,128]{2,1,0:T(8,128)}), f32[8,64,128]{2,1,0:T(8,128)S(1)}, u32[]{:S(2)}, u32[]{:S(2)}) async-start(f32[8,64,128]{2,1,0:T(8,128)} %bitcast.3), calls=%async_computation | async-start | bytes 524288 | tf_op jit(solution)/shard_map/all_to_all | solution.py:476
  13.5 12.3 %copy-start.3 = (bf16[1,6,128,128]{3,2,1,0:T(8,128)(2,1)S(1)}, bf16[1,6,128,128]{3,2,1,0:T(8,128)(2,1)}, u32[]{:S(2)}) copy-start(bf16[1,6,128,128]{3,2,1,0:T(8,128)(2,1)} %fine_ref.1) | copy-start | bytes 589828
  25.7 1.6 %copy-start = (bf16[60,128,128]{2,1,0:T(8,128)(2,1)S(1)}, bf16[60,128,128]{2,1,0:T(8,128)(2,1)}, u32[]{:S(2)}) copy-start(bf16[60,128,128]{2,1,0:T(8,128)(2,1)} %coarse_ref.1) | copy-start | bytes 5898244
  26.1 20.4 %copy-start.1 = (bf16[31,2,128,128]{3,2,1,0:T(8,128)(2,1)S(1)}, bf16[31,2,128,128]{3,2,1,0:T(8,128)(2,1)}, u32[]{:S(2)}) copy-start(bf16[31,2,128,128]{3,2,1,0:T(8,128)(2,1)} %couple_ref.1) | copy-start | bytes 6094852
  26.1 20.4 %copy-start.2 = (bf16[1,7,2,128,128]{4,3,2,1,0:T(8,128)(2,1)S(1)}, bf16[1,7,2,128,128]{4,3,2,1,0:T(8,128)(2,1)}, u32[]{:S(2)}) copy-start(bf16[1,7,2,128,128]{4,3,2,1,0:T(8,128)(2,1)} %refs_2_.1) | copy-start | bytes 1376260
  26.1 1.3 %collective-permute-start = (f32[64,128]{1,0:T(8,128)S(1)}, f32[64,128]{1,0:T(8,128)S(1)}, u32[]{:S(2)}, u32[]{:S(2)}) collective-permute-start(f32[64,128]{1,0:T(8,128)S(1)} %get-tuple-element.34.own_ref), channel_id=1, source_target_pairs={{0,8},{8,0},{16,24},{24,16},{32,40},{40,32},{48,56},{56,48},{64,72... | collective-permute-start | bytes 98312 | tf_op jit(solution)/shard_map/ppermute | solution.py:463
  28.1 21.1 %collective-permute-start.1 = (f32[512,128]{1,0:T(8,128)S(1)}, f32[512,128]{1,0:T(8,128)S(1)}, u32[]{:S(2)}, u32[]{:S(2)}) collective-permute-start(f32[512,128]{1,0:T(8,128)S(1)} %get-tuple-element.36), channel_id=1, source_target_pairs={{0,1},{1,0},{2,3},{3,2},{4,5},{5,4},{6,7},{7,6},{8,9},{9,8},{10,11... | collective-permute-start | bytes 786440 | tf_op jit(solution)/shard_map/ppermute | solution.py:463
  30.2 4.1 %collective-permute-start.4 = (f32[64,128]{1,0:T(8,128)S(1)}, f32[64,128]{1,0:T(8,128)S(1)}, u32[]{:S(2)}, u32[]{:S(2)}) collective-permute-start(f32[64,128]{1,0:T(8,128)S(1)} %pair_up.1.own_ref), channel_id=1, source_target_pairs={{0,48},{8,56},{16,32},{24,40},{32,16},{40,24},{48,0},{56,8},{64,11... | collective-permute-start | bytes 98312 | tf_op jit(solution)/shard_map/ppermute | solution.py:463
  30.6 5.4 %collective-permute-start.3 = (f32[64,128]{1,0:T(8,128)S(1)}, f32[64,128]{1,0:T(8,128)S(1)}, u32[]{:S(2)}, u32[]{:S(2)}) collective-permute-start(f32[64,128]{1,0:T(8,128)S(1)} %pair_up.1.own_ref), channel_id=1, source_target_pairs={{0,32},{8,40},{16,48},{24,56},{32,0},{40,8},{48,16},{56,24},{64,96... | collective-permute-start | bytes 98312 | tf_op jit(solution)/shard_map/ppermute | solution.py:463
  33.5 3.9 %collective-permute-start.2 = (f32[64,128]{1,0:T(8,128)S(1)}, f32[64,128]{1,0:T(8,128)S(1)}, u32[]{:S(2)}, u32[]{:S(2)}) collective-permute-start(f32[64,128]{1,0:T(8,128)S(1)} %pair_up.1.own_ref), channel_id=1, source_target_pairs={{0,16},{8,24},{16,0},{24,8},{32,48},{40,56},{48,32},{56,40},{64,80... | collective-permute-start | bytes 98312 | tf_op jit(solution)/shard_map/ppermute | solution.py:463
  38.3 5.1 %collective-permute-start.7 = (f32[64,128]{1,0:T(8,128)S(1)}, f32[64,128]{1,0:T(8,128)S(1)}, u32[]{:S(2)}, u32[]{:S(2)}) collective-permute-start(f32[64,128]{1,0:T(8,128)S(1)} %get-tuple-element.38.top_ref), channel_id=1, source_target_pairs={{0,192},{8,200},{16,208},{24,216},{32,224},{40,232},{48,240},{56,2... | collective-permute-start | bytes 98312 | tf_op jit(solution)/shard_map/ppermute | solution.py:463
  41.1 5.4 %collective-permute-start.6 = (f32[64,128]{1,0:T(8,128)S(1)}, f32[64,128]{1,0:T(8,128)S(1)}, u32[]{:S(2)}, u32[]{:S(2)}) collective-permute-start(f32[64,128]{1,0:T(8,128)S(1)} %get-tuple-element.38.top_ref), channel_id=1, source_target_pairs={{0,128},{8,136},{16,144},{24,152},{32,160},{40,168},{48,176},{56,1... | collective-permute-start | bytes 98312 | tf_op jit(solution)/shard_map/ppermute | solution.py:463
  41.9 4.6 %collective-permute-start.5 = (f32[64,128]{1,0:T(8,128)S(1)}, f32[64,128]{1,0:T(8,128)S(1)}, u32[]{:S(2)}, u32[]{:S(2)}) collective-permute-start(f32[64,128]{1,0:T(8,128)S(1)} %get-tuple-element.38.top_ref), channel_id=1, source_target_pairs={{0,64},{8,72},{16,80},{24,88},{32,96},{40,104},{48,112},{56,120},{... | collective-permute-start | bytes 98312 | tf_op jit(solution)/shard_map/ppermute | solution.py:463
  49.2 20.5 %all-to-all-start.1 = ((f32[8,128,128]{2,1,0:T(8,128)}), f32[8,128,128]{2,1,0:T(8,128)S(1)}, u32[]{:S(2)}, u32[]{:S(2)}) async-start(f32[8,128,128]{2,1,0:T(8,128)} %turn.1), calls=%async_computation.1 | async-start | bytes 1048576 | tf_op jit(solution)/shard_map/all_to_all | solution.py:505
where the time goes:
time: 74.6 us; the launch traced here: 74.3 us
  Pallas kernels  38 us (51%)
  starting transfers between devices  24.6 us (33%)
  waiting for transfers between devices  10.7 us (14%)
  between operations  0.92 us (1%)
    pallas_call x2, Pallas kernels, near_part(): pl.pallas_call(functools.partial(near_kernel, first=first), grid=(count,)...  24.7 us
    ppermute x8, starting transfers between devices, swap(): lax.ppermute(x, axis, [(i, i ^ mask) for i in range(lax.axis_size(axis))])  10.4 us
    all_to_all x1, starting transfers between devices, per_device(): lax.all_to_all(lift_t.reshape(group, columns // group, rank), 'gy', 0, 0)  8.47 us
    ppermute x8, waiting for transfers between devices, swap(): lax.ppermute(x, axis, [(i, i ^ mask) for i in range(lax.axis_size(axis))])  8.37 us
    all_to_all x1, starting transfers between devices, per_device(): down = lax.all_to_all(sent, 'gy', 0, 0)  5.75 us
    pallas_call x1, Pallas kernels, finish(): pl.pallas_call(finish_kernel, out_shape=(shape, shape), in_specs=vmem(1)...  4.4 us
    pallas_call x1, Pallas kernels, leaf_up(): pl.pallas_call(leaf_up_kernel, out_shape=(shape, shape), in_specs=hbm(4),...  4.33 us
    pallas_call x1, Pallas kernels, turn(): pl.pallas_call(turn_kernel, out_shape=jax.ShapeDtypeStruct((8, 2 * column...  2.71 us
  transfers between devices with their start and end apart: 10, of which 6 were waited for; matrix products, arithmetic and copies ran while one was open for 0% of the time, Pallas kernels for 38%

commit v1 on v0

--- a/solution.py
+++ b/solution.py
@@ -118,7 +118,9 @@
     h_t = jnp.transpose(dot_nn(stored_ref[...], probes_ref[...]))
     copies[3].wait()
     h_ref[...] = h_t
-    lift_ref[...] = exact(dot_nn, h_t, transfer_ref[0])
+    half = h_t.shape[0] // 2
+    for part in (0, half):
+        lift_ref[part : part + half, :] = exact(dot_nn, h_t[part : part + half], transfer_ref[0])
 
 
 def leaf_up(order, basis, probes, transfer):
@@ -188,8 +190,16 @@
 
     columns = order_columns(order_ref, first + block * rows, rows)
     hot_ref[...] = one_hot(columns, 0, leaf)
-    rows_left = dot_nt(hot_ref[...], left_ref[...]).astype(bf16)
-    basis = basis_ref[...]
+    half = rows // 2
+    rows_left = jnp.concatenate(
+        [dot_nt(hot_ref[part : part + half, :], left_ref[...]) for part in (0, half)], axis=0
+    ).astype(bf16)
+
+    @pl.when(block == 0)
+    def _():
+        copy.wait()
+
+    basis = basis_ref[pl.ds(pl.multiple_of(first + block * rows, 128), rows), :]
     rank = basis.shape[1]
     wide_ref[:, :rank] = dot_nn(basis, transfer_ref[0]).astype(bf16)
     wide_ref[:, rank:] = basis
@@ -201,10 +211,6 @@
         both_ref[0:rows, pl.ds(start, step)] = ((1.0 + root * slope) * falloff).astype(bf16)
         both_ref[rows : 2 * rows, pl.ds(start, step)] = (squared * falloff).astype(bf16)
 
-    @pl.when(block == 0)
-    def _():
-        copy.wait()
-
     sums = dot_nn(both_ref[...], probes_ref[...])
     kernel_ref[...] = sums[:rows].astype(bf16)
     derivative_ref[...] = (sums[rows:] * (slope * slope)).astype(bf16)
@@ -213,7 +219,6 @@
 def near_part(order, points, transfer, basis, probes, extra, first, count, rows):
     leaf, columns = probes.shape
     rank = basis.shape[1]
-    held = first // rows
     out_shape = [pltpu.HBM((count * rows, width), bf16) for width in (columns, columns, 2 * rank)]
     out_specs = [pl.BlockSpec((rows, width), lambda i: (i, 0)) for width in (columns, columns, 2 * rank)]
     extra_specs = []
@@ -232,7 +237,7 @@
             pl.BlockSpec(order.shape, whole),
             pl.BlockSpec(points.shape, whole),
             pl.BlockSpec(transfer.shape, lambda i: (0, 0, 0)),
-            pl.BlockSpec((rows, rank), lambda i: (held + i, 0)),
+            pl.BlockSpec(basis.shape, whole),
             pl.BlockSpec(memory_space=pltpu.HBM),
         ]
         + extra_specs,
@@ -247,7 +252,7 @@
         ],
         compiler_params=params(32),
         cost_estimate=cost(2.0 * count * rows * leaf * (columns * 2 + 512), 6 * MIB),
-    )(order, points, transfer, *held_in_hbm(basis, probes), *extra)
+    )(*held_in_hbm(order, points, transfer, basis, probes), *extra)
 
 
 def fine_up_kernel(lift_ref, transfer_ref, one_ref, two_ref, three_ref):
@@ -474,8 +479,8 @@
     leaf = probes.shape[0]
     order_a, lift_t = lax.optimization_barrier((order, lift_t))
     lifts = lax.all_to_all(lift_t.reshape(group, columns // group, rank), "gy", 0, 0)
-    rows = leaf // 4
-    near_a = near_part(order_a, points_t, leaf_transfer, leaf_basis, probes, (), 0, 2, rows)
+    rows = leaf // 16
+    near_a = near_part(order_a, points_t, leaf_transfer, leaf_basis, probes, (), 0, 2, 4 * rows)
     near_a, lifts = lax.optimization_barrier((near_a, lifts))
     one, two, three = fine_up(lifts, fine_transfer)
     three_sibling = swap(three, "gx", 1)
@@ -503,8 +508,8 @@
     )
     order_b, leaf_sibling, sent = lax.optimization_barrier((order, leaf_sibling, sent))
     down = lax.all_to_all(sent, "gy", 0, 0)
-    extra = (place, leaf_sibling, fine_couple)
-    near_b = near_part(order_b, points_t, leaf_transfer, leaf_basis, probes, extra, 2 * rows, 2, rows)
+    extra = (place, leaf_sibling, *held_in_hbm(fine_couple))
+    near_b = near_part(order_b, points_t, leaf_transfer, leaf_basis, probes, extra, 8 * rows, 2, 4 * rows)
     return finish(down, near_b[3], *near_a, *near_b[:3])
 
 

time: 74.6 us -> 73.2 us (0.981)
  Pallas kernels: 38 us -> 35.2 us
  waiting for transfers between devices: 10.7 us -> 13 us
  starting transfers between devices: 24.6 us -> 23.6 us
    pallas_call x2, Pallas kernels: 24.7 us -> 22 us  [near_part(): pl.pallas_call(functools.partial(near_kernel, first=first), grid=(count,)...]
    all_to_all x1, waiting for transfers between devices: 2.29 us -> 3.68 us  [per_device(): down = lax.all_to_all(sent, 'gy', 0, 0)]
    all_to_all x1, waiting for transfers between devices: 0.01 us -> 0.99 us  [per_device(): lax.all_to_all(lift_t.reshape(group, columns // group, rank), 'gy', 0, 0)]
    ppermute x8, starting transfers between devices: 10.4 us -> 9.42 us  [swap(): lax.ppermute(x, axis, [(i, i ^ mask) for i in range(lax.axis_size(axis))])]
  transfers between devices with their start and end apart: 10 -> 10, of which waited for: 6 -> 7; matrix products, arithmetic and copies ran while one was open for 0% -> 0% of each run, Pallas kernels for 38% -> 35%
where the time goes in v1:
time: 73.2 us; the launch traced here: 72.8 us
  Pallas kernels  35.2 us (48%)
  starting transfers between devices  23.6 us (32%)
  waiting for transfers between devices  13 us (18%)
  between operations  0.85 us (1%)
    pallas_call x2, Pallas kernels, near_part(): pl.pallas_call(functools.partial(near_kernel, first=first), grid=(count,)...  22 us
    ppermute x8, starting transfers between devices, swap(): lax.ppermute(x, axis, [(i, i ^ mask) for i in range(lax.axis_size(axis))])  9.42 us
    all_to_all x1, starting transfers between devices, per_device(): lax.all_to_all(lift_t.reshape(group, columns // group, rank), 'gy', 0, 0)  8.47 us
    ppermute x8, waiting for transfers between devices, swap(): lax.ppermute(x, axis, [(i, i ^ mask) for i in range(lax.axis_size(axis))])  8.37 us
    all_to_all x1, starting transfers between devices, per_device(): down = lax.all_to_all(sent, 'gy', 0, 0)  5.75 us
    pallas_call x1, Pallas kernels, finish(): pl.pallas_call(finish_kernel, out_shape=(shape, shape), in_specs=vmem(1)...  4.41 us
    pallas_call x1, Pallas kernels, leaf_up(): pl.pallas_call(leaf_up_kernel, out_shape=(shape, shape), in_specs=hbm(4),...  4.28 us
    all_to_all x1, waiting for transfers between devices, per_device(): down = lax.all_to_all(sent, 'gy', 0, 0)  3.68 us
  transfers between devices with their start and end apart: 10, of which 7 were waited for; matrix products, arithmetic and copies ran while one was open for 0% of the time, Pallas kernels for 35%

profile of v1, /device:TPU:16, one launch (start us, length us, event | category | flops | bytes accessed | tf_op | source)
XLA Modules:
  0.0 72.8 jit_solution(2557881730310690587)
XLA Ops:
  0.6 4.3 %leaf_up.1 = (f32[512,128]{1,0:T(8,128)S(1)}, f32[512,128]{1,0:T(8,128)}) custom-call(s32[1,2048]{1,0:T(1,128)} %order_ref.1, bf16[2048,128]{1,0:T(8,128)(2,1)} %basis_ref.3, bf16[2048,512]{1,0:T(8,128)(2,1)} %probes_hbm.5, bf16[1,128,128]{2,1,0:T(8,128)(2,1)} %transfer_ref.9), custom_call_target="tpu_custom_call" | custom-call | flops 4000000000 | bytes 3145728 | tf_op jit(solution)/shard_map/leaf_up/pallas_call | solution.py:130
  4.9 8.5 %all-to-all-start = ((f32[8,64,128]{2,1,0:T(8,128)}), f32[8,64,128]{2,1,0:T(8,128)S(1)}, u32[]{:S(2)}, u32[]{:S(2)}) async-start(f32[8,64,128]{2,1,0:T(8,128)} %bitcast.3), calls=%async_computation | async-start | bytes 524288 | tf_op jit(solution)/shard_map/all_to_all | solution.py:481
  13.4 0.0 copy-start.3
  13.4 10.9 %shard_map.104 = (bf16[1024,512]{1,0:T(8,128)(2,1)}, bf16[1024,512]{1,0:T(8,128)(2,1)}, bf16[1024,256]{1,0:T(8,128)(2,1)}) custom-call(s32[1,2048]{1,0:T(1,128)} %order_ref.1, bf16[64,2048]{1,0:T(8,128)(2,1)} %bitcast.4, bf16[1,128,128]{2,1,0:T(8,128)(2,1)} %transfer_ref.9, bf16[2048,128]{1,0:T(8,128)(2,1)} %basis_ref.3, bf16[2048,512]{1,0:T(8,128)(2,1)} %probes_hbm.5), custom_call_target="tpu_custom_call" | custom-call | flops 6442450944 | bytes 6291456 | tf_op jit(solution)/shard_map/pallas_call | solution.py:232
  24.3 0.0 copy-start
  24.3 1.0 %all-to-all-done.lift_ref = f32[8,64,128]{2,1,0:T(8,128)S(1)} async-done(((f32[8,64,128]{2,1,0:T(8,128)}), f32[8,64,128]{2,1,0:T(8,128)S(1)}, u32[]{:S(2)}, u32[]{:S(2)}) %all-to-all-start) | async-done | bytes 262176 | tf_op jit(solution)/shard_map/all_to_all | solution.py:481
  25.3 0.0 copy-done.3
  25.3 0.3 fine_up.1
  25.6 0.0 copy-start.1
  25.6 0.0 copy-start.2
  25.6 0.1 collective-permute-start
  25.7 0.1 pad_add_fusion.place_ref.refs_0_
  25.8 1.1 %collective-permute-done.other_ref.three_ref = f32[64,128]{1,0:T(8,128)S(1)} collective-permute-done((f32[64,128]{1,0:T(8,128)S(1)}, f32[64,128]{1,0:T(8,128)S(1)}, u32[]{:S(2)}, u32[]{:S(2)}) %collective-permute-start) | collective-permute-done | bytes 32800 | tf_op jit(solution)/shard_map/ppermute | solution.py:468
  26.9 0.0 copy-done
  26.9 0.7 pair_up.1.own_ref
  27.6 1.1 %collective-permute-start.1 = (f32[512,128]{1,0:T(8,128)S(1)}, f32[512,128]{1,0:T(8,128)S(1)}, u32[]{:S(2)}, u32[]{:S(2)}) collective-permute-start(f32[512,128]{1,0:T(8,128)S(1)} %get-tuple-element.36), channel_id=1, source_target_pairs={{0,1},{1,0},{2,3},{3,2},{4,5},{5,4},{6,7},{7,6},{8,9},{9,8},{10,11... | collective-permute-start | bytes 786440 | tf_op jit(solution)/shard_map/ppermute | solution.py:468
  28.7 0.4 collective-permute-start.4
  29.1 2.9 %collective-permute-start.3 = (f32[64,128]{1,0:T(8,128)S(1)}, f32[64,128]{1,0:T(8,128)S(1)}, u32[]{:S(2)}, u32[]{:S(2)}) collective-permute-start(f32[64,128]{1,0:T(8,128)S(1)} %pair_up.1.own_ref), channel_id=1, source_target_pairs={{0,32},{8,40},{16,48},{24,56},{32,0},{40,8},{48,16},{56,24},{64,96... | collective-permute-start | bytes 98312 | tf_op jit(solution)/shard_map/ppermute | solution.py:468
  32.0 0.7 %collective-permute-start.2 = (f32[64,128]{1,0:T(8,128)S(1)}, f32[64,128]{1,0:T(8,128)S(1)}, u32[]{:S(2)}, u32[]{:S(2)}) collective-permute-start(f32[64,128]{1,0:T(8,128)S(1)} %pair_up.1.own_ref), channel_id=1, source_target_pairs={{0,16},{8,24},{16,0},{24,8},{32,48},{40,56},{48,32},{56,40},{64,80... | collective-permute-start | bytes 98312 | tf_op jit(solution)/shard_map/ppermute | solution.py:468
  32.8 0.0 collective-permute-done.4.x3_ref
  32.8 1.8 %collective-permute-done.3.x2_ref = f32[64,128]{1,0:T(8,128)S(1)} collective-permute-done((f32[64,128]{1,0:T(8,128)S(1)}, f32[64,128]{1,0:T(8,128)S(1)}, u32[]{:S(2)}, u32[]{:S(2)}) %collective-permute-start.3) | collective-permute-done | bytes 32800 | tf_op jit(solution)/shard_map/ppermute | solution.py:468
  34.6 1.4 %collective-permute-done.2.x1_ref.four_ref = f32[64,128]{1,0:T(8,128)S(1)} collective-permute-done((f32[64,128]{1,0:T(8,128)S(1)}, f32[64,128]{1,0:T(8,128)S(1)}, u32[]{:S(2)}, u32[]{:S(2)}) %collective-permute-start.2) | collective-permute-done | bytes 32800 | tf_op jit(solution)/shard_map/ppermute | solution.py:468
  36.0 0.9 %quad_up.1 = (f32[64,128]{1,0:T(8,128)S(1)}, f32[64,128]{1,0:T(8,128)S(1)}) custom-call(s32[2]{0:T(128)S(1)} %pad_add_fusion.place_ref.refs_0_, f32[64,128]{1,0:T(8,128)S(1)} %pair_up.1.own_ref, f32[64,128]{1,0:T(8,128)S(1)} %collective-permute-done.2.x1_ref.four_ref, f32[64,128]{1,0:T(8,128)S(1)} %collective-permute-done.3.x2_ref, ...), custom_call_target="tpu_custom_call" | custom-call | flops 100000000 | bytes 131072 | tf_op jit(solution)/shard_map/quad_up/pallas_call | solution.py:325
  36.8 2.8 %collective-permute-start.7 = (f32[64,128]{1,0:T(8,128)S(1)}, f32[64,128]{1,0:T(8,128)S(1)}, u32[]{:S(2)}, u32[]{:S(2)}) collective-permute-start(f32[64,128]{1,0:T(8,128)S(1)} %get-tuple-element.38.top_ref), channel_id=1, source_target_pairs={{0,192},{8,200},{16,208},{24,216},{32,224},{40,232},{48,240},{56,2... | collective-permute-start | bytes 98312 | tf_op jit(solution)/shard_map/ppermute | solution.py:468
  39.6 0.8 %collective-permute-start.6 = (f32[64,128]{1,0:T(8,128)S(1)}, f32[64,128]{1,0:T(8,128)S(1)}, u32[]{:S(2)}, u32[]{:S(2)}) collective-permute-start(f32[64,128]{1,0:T(8,128)S(1)} %get-tuple-element.38.top_ref), channel_id=1, source_target_pairs={{0,128},{8,136},{16,144},{24,152},{32,160},{40,168},{48,176},{56,1... | collective-permute-start | bytes 98312 | tf_op jit(solution)/shard_map/ppermute | solution.py:468
  40.4 0.5 collective-permute-start.5
  40.9 1.0 %collective-permute-done.7.x3_ref = f32[64,128]{1,0:T(8,128)S(1)} collective-permute-done((f32[64,128]{1,0:T(8,128)S(1)}, f32[64,128]{1,0:T(8,128)S(1)}, u32[]{:S(2)}, u32[]{:S(2)}) %collective-permute-start.7) | collective-permute-done | bytes 32800 | tf_op jit(solution)/shard_map/ppermute | solution.py:468
  42.0 3.0 %collective-permute-done.6.x2_ref = f32[64,128]{1,0:T(8,128)S(1)} collective-permute-done((f32[64,128]{1,0:T(8,128)S(1)}, f32[64,128]{1,0:T(8,128)S(1)}, u32[]{:S(2)}, u32[]{:S(2)}) %collective-permute-start.6) | collective-permute-done | bytes 32800 | tf_op jit(solution)/shard_map/ppermute | solution.py:468
  45.0 0.0 collective-permute-done.5.x1_ref
  45.0 0.0 copy-done.1
  45.0 0.0 copy-done.2
  45.0 2.7 %turn.1 = f32[8,128,128]{2,1,0:T(8,128)} custom-call(s32[2]{0:T(128)S(1)} %pad_add_fusion.place_ref.refs_0_, f32[64,128]{1,0:T(8,128)S(1)} %get-tuple-element.38.top_ref, f32[64,128]{1,0:T(8,128)S(1)} %collective-permute-done.5.x1_ref, f32[64,128]{1,0:T(8,128)S(1)} %collective-permute-done.6.x2_ref, f32[64,128]{1,0:T(8,128)S(1)} %collective-permute-done.7.x3_ref, ...), custom_call_target="tpu_custom_call" | custom-call | flops 1000000000 | bytes 1048576 | tf_op jit(solution)/shard_map/turn/pallas_call | solution.py:391
  47.7 0.0 collective-permute-done.1.refs_1_
  47.7 5.8 %all-to-all-start.1 = ((f32[8,128,128]{2,1,0:T(8,128)}), f32[8,128,128]{2,1,0:T(8,128)S(1)}, u32[]{:S(2)}, u32[]{:S(2)}) async-start(f32[8,128,128]{2,1,0:T(8,128)} %turn.1), calls=%async_computation.1 | async-start | bytes 1048576 | tf_op jit(solution)/shard_map/all_to_all | solution.py:510
  53.5 11.1 %shard_map.105 = (bf16[1024,512]{1,0:T(8,128)(2,1)}, bf16[1024,512]{1,0:T(8,128)(2,1)}, bf16[1024,256]{1,0:T(8,128)(2,1)}, bf16[2,512,128]{2,1,0:T(8,128)(2,1)}) custom-call(s32[1,2048]{1,0:T(1,128)} %order_ref.1, bf16[64,2048]{1,0:T(8,128)(2,1)} %bitcast.5, bf16[1,128,128]{2,1,0:T(8,128)(2,1)} %transfer_ref.9, bf16[2048,128]{1,0:T(8,128)(2,1)} %basis_ref.3, ...), custom_call_target="tpu_custom_call" | custom-call | flops 6442450944 | bytes 6291456 | tf_op jit(solution)/shard_map/pallas_call | solution.py:232
  64.6 3.7 %all-to-all-done.1.down_ref = f32[8,128,128]{2,1,0:T(8,128)S(1)} async-done(((f32[8,128,128]{2,1,0:T(8,128)}), f32[8,128,128]{2,1,0:T(8,128)S(1)}, u32[]{:S(2)}, u32[]{:S(2)}) %all-to-all-start.1) | async-done | bytes 524320 | tf_op jit(solution)/shard_map/all_to_all | solution.py:510
  68.3 4.4 %finish.1 = (bf16[2048,512]{1,0:T(8,128)(2,1)}, bf16[2048,512]{1,0:T(8,128)(2,1)}) custom-call(f32[8,128,128]{2,1,0:T(8,128)S(1)} %all-to-all-done.1.down_ref, bf16[2,512,128]{2,1,0:T(8,128)(2,1)} %get-tuple-element.45.couple_hbm, bf16[1024,512]{1,0:T(8,128)(2,1)} %get-tuple-element.46.refs_0_, bf16[1024,512]{1,0:T(8,128)(2,1)} %get-tuple-element.47.refs_1_, ...), custom_call_target="tpu_custom_call" | custom-call | flops 1000000000 | bytes 10485760 | tf_op jit(solution)/shard_map/finish/pallas_call | solution.py:448
Async XLA Ops:
  4.9 20.4 %all-to-all-start = ((f32[8,64,128]{2,1,0:T(8,128)}), f32[8,64,128]{2,1,0:T(8,128)S(1)}, u32[]{:S(2)}, u32[]{:S(2)}) async-start(f32[8,64,128]{2,1,0:T(8,128)} %bitcast.3), calls=%async_computation | async-start | bytes 524288 | tf_op jit(solution)/shard_map/all_to_all | solution.py:481
  13.4 11.9 %copy-start.3 = (bf16[1,6,128,128]{3,2,1,0:T(8,128)(2,1)S(1)}, bf16[1,6,128,128]{3,2,1,0:T(8,128)(2,1)}, u32[]{:S(2)}) copy-start(bf16[1,6,128,128]{3,2,1,0:T(8,128)(2,1)} %fine_ref.1) | copy-start | bytes 589828
  24.3 2.6 %copy-start = (bf16[60,128,128]{2,1,0:T(8,128)(2,1)S(1)}, bf16[60,128,128]{2,1,0:T(8,128)(2,1)}, u32[]{:S(2)}) copy-start(bf16[60,128,128]{2,1,0:T(8,128)(2,1)} %coarse_ref.1) | copy-start | bytes 5898244
  25.6 19.4 %copy-start.1 = (bf16[31,2,128,128]{3,2,1,0:T(8,128)(2,1)S(1)}, bf16[31,2,128,128]{3,2,1,0:T(8,128)(2,1)}, u32[]{:S(2)}) copy-start(bf16[31,2,128,128]{3,2,1,0:T(8,128)(2,1)} %couple_ref.1) | copy-start | bytes 6094852
  25.6 19.4 %copy-start.2 = (bf16[1,7,2,128,128]{4,3,2,1,0:T(8,128)(2,1)S(1)}, bf16[1,7,2,128,128]{4,3,2,1,0:T(8,128)(2,1)}, u32[]{:S(2)}) copy-start(bf16[1,7,2,128,128]{4,3,2,1,0:T(8,128)(2,1)} %refs_2_.1) | copy-start | bytes 1376260
  25.6 1.3 %collective-permute-start = (f32[64,128]{1,0:T(8,128)S(1)}, f32[64,128]{1,0:T(8,128)S(1)}, u32[]{:S(2)}, u32[]{:S(2)}) collective-permute-start(f32[64,128]{1,0:T(8,128)S(1)} %get-tuple-element.34.own_ref), channel_id=1, source_target_pairs={{0,8},{8,0},{16,24},{24,16},{32,40},{40,32},{48,56},{56,48},{64,72... | collective-permute-start | bytes 98312 | tf_op jit(solution)/shard_map/ppermute | solution.py:468
  27.6 20.2 %collective-permute-start.1 = (f32[512,128]{1,0:T(8,128)S(1)}, f32[512,128]{1,0:T(8,128)S(1)}, u32[]{:S(2)}, u32[]{:S(2)}) collective-permute-start(f32[512,128]{1,0:T(8,128)S(1)} %get-tuple-element.36), channel_id=1, source_target_pairs={{0,1},{1,0},{2,3},{3,2},{4,5},{5,4},{6,7},{7,6},{8,9},{9,8},{10,11... | collective-permute-start | bytes 786440 | tf_op jit(solution)/shard_map/ppermute | solution.py:468
  28.7 4.1 %collective-permute-start.4 = (f32[64,128]{1,0:T(8,128)S(1)}, f32[64,128]{1,0:T(8,128)S(1)}, u32[]{:S(2)}, u32[]{:S(2)}) collective-permute-start(f32[64,128]{1,0:T(8,128)S(1)} %pair_up.1.own_ref), channel_id=1, source_target_pairs={{0,48},{8,56},{16,32},{24,40},{32,16},{40,24},{48,0},{56,8},{64,11... | collective-permute-start | bytes 98312 | tf_op jit(solution)/shard_map/ppermute | solution.py:468
  29.1 5.4 %collective-permute-start.3 = (f32[64,128]{1,0:T(8,128)S(1)}, f32[64,128]{1,0:T(8,128)S(1)}, u32[]{:S(2)}, u32[]{:S(2)}) collective-permute-start(f32[64,128]{1,0:T(8,128)S(1)} %pair_up.1.own_ref), channel_id=1, source_target_pairs={{0,32},{8,40},{16,48},{24,56},{32,0},{40,8},{48,16},{56,24},{64,96... | collective-permute-start | bytes 98312 | tf_op jit(solution)/shard_map/ppermute | solution.py:468
  32.0 3.9 %collective-permute-start.2 = (f32[64,128]{1,0:T(8,128)S(1)}, f32[64,128]{1,0:T(8,128)S(1)}, u32[]{:S(2)}, u32[]{:S(2)}) collective-permute-start(f32[64,128]{1,0:T(8,128)S(1)} %pair_up.1.own_ref), channel_id=1, source_target_pairs={{0,16},{8,24},{16,0},{24,8},{32,48},{40,56},{48,32},{56,40},{64,80... | collective-permute-start | bytes 98312 | tf_op jit(solution)/shard_map/ppermute | solution.py:468
  36.8 5.1 %collective-permute-start.7 = (f32[64,128]{1,0:T(8,128)S(1)}, f32[64,128]{1,0:T(8,128)S(1)}, u32[]{:S(2)}, u32[]{:S(2)}) collective-permute-start(f32[64,128]{1,0:T(8,128)S(1)} %get-tuple-element.38.top_ref), channel_id=1, source_target_pairs={{0,192},{8,200},{16,208},{24,216},{32,224},{40,232},{48,240},{56,2... | collective-permute-start | bytes 98312 | tf_op jit(solution)/shard_map/ppermute | solution.py:468
  39.6 5.4 %collective-permute-start.6 = (f32[64,128]{1,0:T(8,128)S(1)}, f32[64,128]{1,0:T(8,128)S(1)}, u32[]{:S(2)}, u32[]{:S(2)}) collective-permute-start(f32[64,128]{1,0:T(8,128)S(1)} %get-tuple-element.38.top_ref), channel_id=1, source_target_pairs={{0,128},{8,136},{16,144},{24,152},{32,160},{40,168},{48,176},{56,1... | collective-permute-start | bytes 98312 | tf_op jit(solution)/shard_map/ppermute | solution.py:468
  40.4 4.6 %collective-permute-start.5 = (f32[64,128]{1,0:T(8,128)S(1)}, f32[64,128]{1,0:T(8,128)S(1)}, u32[]{:S(2)}, u32[]{:S(2)}) collective-permute-start(f32[64,128]{1,0:T(8,128)S(1)} %get-tuple-element.38.top_ref), channel_id=1, source_target_pairs={{0,64},{8,72},{16,80},{24,88},{32,96},{40,104},{48,112},{56,120},{... | collective-permute-start | bytes 98312 | tf_op jit(solution)/shard_map/ppermute | solution.py:468
  47.7 20.5 %all-to-all-start.1 = ((f32[8,128,128]{2,1,0:T(8,128)}), f32[8,128,128]{2,1,0:T(8,128)S(1)}, u32[]{:S(2)}, u32[]{:S(2)}) async-start(f32[8,128,128]{2,1,0:T(8,128)} %turn.1), calls=%async_computation.1 | async-start | bytes 1048576 | tf_op jit(solution)/shard_map/all_to_all | solution.py:510

commit v2 on v1

--- a/solution.py
+++ b/solution.py
@@ -252,7 +252,7 @@
         ],
         compiler_params=params(32),
         cost_estimate=cost(2.0 * count * rows * leaf * (columns * 2 + 512), 6 * MIB),
-    )(*held_in_hbm(order, points, transfer, basis, probes), *extra)
+    )(order, points, transfer, *held_in_hbm(basis, probes), *extra)
 
 
 def fine_up_kernel(lift_ref, transfer_ref, one_ref, two_ref, three_ref):
@@ -405,12 +405,10 @@
     part = down_ref.shape[1] // 2
     arrivals = [pltpu.make_async_copy(couple_hbm, couple_ref, in_sems.at[0])]
     spans = []
-    start = 0
-    for half in range(2):
+    for half in (1, 0):
         near_k, near_d, wide = parts_hbm[3 * half : 3 * half + 3]
-        span = pl.ds(start, near_k.shape[0])
+        span = pl.ds(half * parts_hbm[0].shape[0], near_k.shape[0])
         spans.append(span)
-        start += near_k.shape[0]
         for source, target in (
             (wide, wide_ref.at[span, :]),
             (near_k, near_ref.at[0, span, :]),
@@ -480,7 +478,7 @@
     order_a, lift_t = lax.optimization_barrier((order, lift_t))
     lifts = lax.all_to_all(lift_t.reshape(group, columns // group, rank), "gy", 0, 0)
     rows = leaf // 16
-    near_a = near_part(order_a, points_t, leaf_transfer, leaf_basis, probes, (), 0, 2, 4 * rows)
+    near_a = near_part(order_a, points_t, leaf_transfer, leaf_basis, probes, (), 0, 2, 3 * rows)
     near_a, lifts = lax.optimization_barrier((near_a, lifts))
     one, two, three = fine_up(lifts, fine_transfer)
     three_sibling = swap(three, "gx", 1)
@@ -509,7 +507,7 @@
     order_b, leaf_sibling, sent = lax.optimization_barrier((order, leaf_sibling, sent))
     down = lax.all_to_all(sent, "gy", 0, 0)
     extra = (place, leaf_sibling, *held_in_hbm(fine_couple))
-    near_b = near_part(order_b, points_t, leaf_transfer, leaf_basis, probes, extra, 8 * rows, 2, 4 * rows)
+    near_b = near_part(order_b, points_t, leaf_transfer, leaf_basis, probes, extra, 6 * rows, 2, 5 * rows)
     return finish(down, near_b[3], *near_a, *near_b[:3])
 
 

time: 73.2 us -> 71.4 us (0.975)
  the two profiles are of different devices: /device:TPU:16 before, /device:TPU:64 now
where the time goes in v2:
time: 71.4 us; the launch traced here: 70.1 us
  Pallas kernels  35.4 us (50%)
  starting transfers between devices  24.2 us (34%)
  waiting for transfers between devices  9.57 us (13%)
  between operations  0.91 us (1%)
    pallas_call x2, Pallas kernels, near_part(): pl.pallas_call(functools.partial(near_kernel, first=first), grid=(count,)...  22 us
    ppermute x8, starting transfers between devices, swap(): lax.ppermute(x, axis, [(i, i ^ mask) for i in range(lax.axis_size(axis))])  9.73 us
    ppermute x8, waiting for transfers between devices, swap(): lax.ppermute(x, axis, [(i, i ^ mask) for i in range(lax.axis_size(axis))])  9.57 us
    all_to_all x1, starting transfers between devices, per_device(): lax.all_to_all(lift_t.reshape(group, columns // group, rank), 'gy', 0, 0)  8.12 us
    all_to_all x1, starting transfers between devices, per_device(): down = lax.all_to_all(sent, 'gy', 0, 0)  6.31 us
    pallas_call x1, Pallas kernels, finish(): pl.pallas_call(finish_kernel, out_shape=(shape, shape), in_specs=vmem(1)...  4.46 us
    pallas_call x1, Pallas kernels, leaf_up(): pl.pallas_call(leaf_up_kernel, out_shape=(shape, shape), in_specs=hbm(4),...  4.33 us
    pallas_call x1, Pallas kernels, turn(): pl.pallas_call(turn_kernel, out_shape=jax.ShapeDtypeStruct((8, 2 * column...  2.71 us
  transfers between devices with their start and end apart: 10, of which 5 were waited for; matrix products, arithmetic and copies ran while one was open for 0% of the time, Pallas kernels for 37%

profile of v2, /device:TPU:64, one launch (start us, length us, event | category | flops | bytes accessed | tf_op | source)
XLA Modules:
  0.0 70.1 jit_solution(10026055472583498377)
XLA Ops:
  0.6 0.0 copy-start.5
  0.6 0.0 copy-start.6
  0.6 0.0 copy-start.4
  0.7 4.3 %leaf_up.1 = (f32[512,128]{1,0:T(8,128)S(1)}, f32[512,128]{1,0:T(8,128)}) custom-call(s32[1,2048]{1,0:T(1,128)} %order_ref.1, bf16[2048,128]{1,0:T(8,128)(2,1)} %basis_ref.3, bf16[2048,512]{1,0:T(8,128)(2,1)} %probes_hbm.5, bf16[1,128,128]{2,1,0:T(8,128)(2,1)} %transfer_ref.9), custom_call_target="tpu_custom_call" | custom-call | flops 4000000000 | bytes 3145728 | tf_op jit(solution)/shard_map/leaf_up/pallas_call | solution.py:130
  5.0 8.1 %all-to-all-start = ((f32[8,64,128]{2,1,0:T(8,128)}), f32[8,64,128]{2,1,0:T(8,128)S(1)}, u32[]{:S(2)}, u32[]{:S(2)}) async-start(f32[8,64,128]{2,1,0:T(8,128)} %bitcast.3), calls=%async_computation | async-start | bytes 524288 | tf_op jit(solution)/shard_map/all_to_all | solution.py:479
  13.1 0.0 copy-done.5
  13.1 0.0 copy-done.6
  13.1 0.0 copy-done.4
  13.1 0.0 copy-start.3
  13.1 9.0 %shard_map.104 = (bf16[768,512]{1,0:T(8,128)(2,1)}, bf16[768,512]{1,0:T(8,128)(2,1)}, bf16[768,256]{1,0:T(8,128)(2,1)}) custom-call(s32[1,2048]{1,0:T(1,128)S(1)} %copy-done.6, bf16[64,2048]{1,0:T(8,128)(2,1)S(1)} %bitcast.4, bf16[1,128,128]{2,1,0:T(8,128)(2,1)S(1)} %copy-done.5, bf16[2048,128]{1,0:T(8,128)(2,1)} %basis_ref.3, bf16[2048,512]{1,0:T(8,128)(2,1)} %probes_hbm.5), custom_call_target="tpu_custom_call" | custom-call | flops 4831838208 | bytes 6291456 | tf_op jit(solution)/shard_map/pallas_call | solution.py:232
  22.2 0.0 copy-start
  22.2 0.0 all-to-all-done.lift_ref
  22.2 0.0 copy-done.3
  22.2 0.3 fine_up.1
  22.5 0.0 collective-permute-start
  22.5 0.1 pad_add_fusion.place_ref.refs_0_
  22.6 0.0 copy-start.1
  22.6 0.0 copy-start.2
  22.6 1.1 %collective-permute-done.other_ref.three_ref = f32[64,128]{1,0:T(8,128)S(1)} collective-permute-done((f32[64,128]{1,0:T(8,128)S(1)}, f32[64,128]{1,0:T(8,128)S(1)}, u32[]{:S(2)}, u32[]{:S(2)}) %collective-permute-start) | collective-permute-done | bytes 32800 | tf_op jit(solution)/shard_map/ppermute | solution.py:466
  23.7 0.0 copy-done
  23.7 0.7 pair_up.1.own_ref
  24.4 1.5 %collective-permute-start.1 = (f32[512,128]{1,0:T(8,128)S(1)}, f32[512,128]{1,0:T(8,128)S(1)}, u32[]{:S(2)}, u32[]{:S(2)}) collective-permute-start(f32[512,128]{1,0:T(8,128)S(1)} %get-tuple-element.36), channel_id=1, source_target_pairs={{0,1},{1,0},{2,3},{3,2},{4,5},{5,4},{6,7},{7,6},{8,9},{9,8},{10,11... | collective-permute-start | bytes 786440 | tf_op jit(solution)/shard_map/ppermute | solution.py:466
  25.9 3.0 %collective-permute-start.4 = (f32[64,128]{1,0:T(8,128)S(1)}, f32[64,128]{1,0:T(8,128)S(1)}, u32[]{:S(2)}, u32[]{:S(2)}) collective-permute-start(f32[64,128]{1,0:T(8,128)S(1)} %pair_up.1.own_ref), channel_id=1, source_target_pairs={{0,48},{8,56},{16,32},{24,40},{32,16},{40,24},{48,0},{56,8},{64,11... | collective-permute-start | bytes 98312 | tf_op jit(solution)/shard_map/ppermute | solution.py:466
  29.0 0.6 collective-permute-start.3
  29.6 0.4 collective-permute-start.2
  30.0 1.0 %collective-permute-done.4.x3_ref = f32[64,128]{1,0:T(8,128)S(1)} collective-permute-done((f32[64,128]{1,0:T(8,128)S(1)}, f32[64,128]{1,0:T(8,128)S(1)}, u32[]{:S(2)}, u32[]{:S(2)}) %collective-permute-start.4) | collective-permute-done | bytes 32800 | tf_op jit(solution)/shard_map/ppermute | solution.py:466
  31.1 3.3 %collective-permute-done.3.x2_ref = f32[64,128]{1,0:T(8,128)S(1)} collective-permute-done((f32[64,128]{1,0:T(8,128)S(1)}, f32[64,128]{1,0:T(8,128)S(1)}, u32[]{:S(2)}, u32[]{:S(2)}) %collective-permute-start.3) | collective-permute-done | bytes 32800 | tf_op jit(solution)/shard_map/ppermute | solution.py:466
  34.4 0.0 collective-permute-done.2.x1_ref.four_ref
  34.4 0.9 %quad_up.1 = (f32[64,128]{1,0:T(8,128)S(1)}, f32[64,128]{1,0:T(8,128)S(1)}) custom-call(s32[2]{0:T(128)S(1)} %pad_add_fusion.place_ref.refs_0_, f32[64,128]{1,0:T(8,128)S(1)} %pair_up.1.own_ref, f32[64,128]{1,0:T(8,128)S(1)} %collective-permute-done.2.x1_ref.four_ref, f32[64,128]{1,0:T(8,128)S(1)} %collective-permute-done.3.x2_ref, ...), custom_call_target="tpu_custom_call" | custom-call | flops 100000000 | bytes 131072 | tf_op jit(solution)/shard_map/quad_up/pallas_call | solution.py:325
  35.2 2.8 %collective-permute-start.7 = (f32[64,128]{1,0:T(8,128)S(1)}, f32[64,128]{1,0:T(8,128)S(1)}, u32[]{:S(2)}, u32[]{:S(2)}) collective-permute-start(f32[64,128]{1,0:T(8,128)S(1)} %get-tuple-element.38.top_ref), channel_id=1, source_target_pairs={{0,192},{8,200},{16,208},{24,216},{32,224},{40,232},{48,240},{56,2... | collective-permute-start | bytes 98312 | tf_op jit(solution)/shard_map/ppermute | solution.py:466
  38.0 0.8 %collective-permute-start.6 = (f32[64,128]{1,0:T(8,128)S(1)}, f32[64,128]{1,0:T(8,128)S(1)}, u32[]{:S(2)}, u32[]{:S(2)}) collective-permute-start(f32[64,128]{1,0:T(8,128)S(1)} %get-tuple-element.38.top_ref), channel_id=1, source_target_pairs={{0,128},{8,136},{16,144},{24,152},{32,160},{40,168},{48,176},{56,1... | collective-permute-start | bytes 98312 | tf_op jit(solution)/shard_map/ppermute | solution.py:466
  38.8 0.5 collective-permute-start.5
  39.3 1.0 %collective-permute-done.7.x3_ref = f32[64,128]{1,0:T(8,128)S(1)} collective-permute-done((f32[64,128]{1,0:T(8,128)S(1)}, f32[64,128]{1,0:T(8,128)S(1)}, u32[]{:S(2)}, u32[]{:S(2)}) %collective-permute-start.7) | collective-permute-done | bytes 32800 | tf_op jit(solution)/shard_map/ppermute | solution.py:466
  40.4 3.0 %collective-permute-done.6.x2_ref = f32[64,128]{1,0:T(8,128)S(1)} collective-permute-done((f32[64,128]{1,0:T(8,128)S(1)}, f32[64,128]{1,0:T(8,128)S(1)}, u32[]{:S(2)}, u32[]{:S(2)}) %collective-permute-start.6) | collective-permute-done | bytes 32800 | tf_op jit(solution)/shard_map/ppermute | solution.py:466
  43.4 0.0 collective-permute-done.5.x1_ref
  43.4 0.0 copy-done.1
  43.4 0.0 copy-done.2
  43.4 2.7 %turn.1 = f32[8,128,128]{2,1,0:T(8,128)} custom-call(s32[2]{0:T(128)S(1)} %pad_add_fusion.place_ref.refs_0_, f32[64,128]{1,0:T(8,128)S(1)} %get-tuple-element.38.top_ref, f32[64,128]{1,0:T(8,128)S(1)} %collective-permute-done.5.x1_ref, f32[64,128]{1,0:T(8,128)S(1)} %collective-permute-done.6.x2_ref, f32[64,128]{1,0:T(8,128)S(1)} %collective-permute-done.7.x3_ref, ...), custom_call_target="tpu_custom_call" | custom-call | flops 1000000000 | bytes 1048576 | tf_op jit(solution)/shard_map/turn/pallas_call | solution.py:391
  46.2 0.0 collective-permute-done.1.refs_1_
  46.2 6.3 %all-to-all-start.1 = ((f32[8,128,128]{2,1,0:T(8,128)}), f32[8,128,128]{2,1,0:T(8,128)S(1)}, u32[]{:S(2)}, u32[]{:S(2)}) async-start(f32[8,128,128]{2,1,0:T(8,128)} %turn.1), calls=%async_computation.1 | async-start | bytes 1048576 | tf_op jit(solution)/shard_map/all_to_all | solution.py:508
  52.5 13.0 %shard_map.105 = (bf16[1280,512]{1,0:T(8,128)(2,1)}, bf16[1280,512]{1,0:T(8,128)(2,1)}, bf16[1280,256]{1,0:T(8,128)(2,1)}, bf16[2,512,128]{2,1,0:T(8,128)(2,1)}) custom-call(s32[1,2048]{1,0:T(1,128)S(1)} %copy-done.6, bf16[64,2048]{1,0:T(8,128)(2,1)S(1)} %bitcast.5, bf16[1,128,128]{2,1,0:T(8,128)(2,1)S(1)} %copy-done.5, bf16[2048,128]{1,0:T(8,128)(2,1)} %basis_ref.3, ...), custom_call_target="tpu_custom_call" | custom-call | flops 8053063680 | bytes 6291456 | tf_op jit(solution)/shard_map/pallas_call | solution.py:232
  65.5 0.0 all-to-all-done.1.down_ref
  65.5 4.5 %finish.1 = (bf16[2048,512]{1,0:T(8,128)(2,1)}, bf16[2048,512]{1,0:T(8,128)(2,1)}) custom-call(f32[8,128,128]{2,1,0:T(8,128)S(1)} %all-to-all-done.1.down_ref, bf16[2,512,128]{2,1,0:T(8,128)(2,1)} %get-tuple-element.45.couple_hbm, bf16[768,512]{1,0:T(8,128)(2,1)} %get-tuple-element.46.refs_0_, bf16[768,512]{1,0:T(8,128)(2,1)} %get-tuple-element.47.refs_1_, ...), custom_call_target="tpu_custom_call" | custom-call | flops 1000000000 | bytes 10485760 | tf_op jit(solution)/shard_map/finish/pallas_call | solution.py:446
Async XLA Ops:
  0.6 12.5 %copy-start.5 = (bf16[1,128,128]{2,1,0:T(8,128)(2,1)S(1)}, bf16[1,128,128]{2,1,0:T(8,128)(2,1)}, u32[]{:S(2)}) copy-start(bf16[1,128,128]{2,1,0:T(8,128)(2,1)} %transfer_ref.9) | copy-start | bytes 98308
  0.6 12.5 %copy-start.6 = (s32[1,2048]{1,0:T(1,128)S(1)}, s32[1,2048]{1,0:T(1,128)}, u32[]{:S(2)}) copy-start(s32[1,2048]{1,0:T(1,128)} %order_ref.1) | copy-start | bytes 24580
  0.6 12.5 %copy-start.4 = (bf16[2048,64]{0,1:T(8,128)(2,1)S(1)}, bf16[2048,64]{0,1:T(8,128)(2,1)}, u32[]{:S(2)}) copy-start(bf16[2048,64]{0,1:T(8,128)(2,1)} %param.9) | copy-start | bytes 786436
  5.0 17.2 %all-to-all-start = ((f32[8,64,128]{2,1,0:T(8,128)}), f32[8,64,128]{2,1,0:T(8,128)S(1)}, u32[]{:S(2)}, u32[]{:S(2)}) async-start(f32[8,64,128]{2,1,0:T(8,128)} %bitcast.3), calls=%async_computation | async-start | bytes 524288 | tf_op jit(solution)/shard_map/all_to_all | solution.py:479
  13.1 9.0 %copy-start.3 = (bf16[1,6,128,128]{3,2,1,0:T(8,128)(2,1)S(1)}, bf16[1,6,128,128]{3,2,1,0:T(8,128)(2,1)}, u32[]{:S(2)}) copy-start(bf16[1,6,128,128]{3,2,1,0:T(8,128)(2,1)} %fine_ref.1) | copy-start | bytes 589828
  22.2 1.6 %copy-start = (bf16[60,128,128]{2,1,0:T(8,128)(2,1)S(1)}, bf16[60,128,128]{2,1,0:T(8,128)(2,1)}, u32[]{:S(2)}) copy-start(bf16[60,128,128]{2,1,0:T(8,128)(2,1)} %coarse_ref.1) | copy-start | bytes 5898244
  22.5 1.2 %collective-permute-start = (f32[64,128]{1,0:T(8,128)S(1)}, f32[64,128]{1,0:T(8,128)S(1)}, u32[]{:S(2)}, u32[]{:S(2)}) collective-permute-start(f32[64,128]{1,0:T(8,128)S(1)} %get-tuple-element.34.own_ref), channel_id=1, source_target_pairs={{0,8},{8,0},{16,24},{24,16},{32,40},{40,32},{48,56},{56,48},{64,72... | collective-permute-start | bytes 98312 | tf_op jit(solution)/shard_map/ppermute | solution.py:466
  22.6 20.8 %copy-start.1 = (bf16[31,2,128,128]{3,2,1,0:T(8,128)(2,1)S(1)}, bf16[31,2,128,128]{3,2,1,0:T(8,128)(2,1)}, u32[]{:S(2)}) copy-start(bf16[31,2,128,128]{3,2,1,0:T(8,128)(2,1)} %couple_ref.1) | copy-start | bytes 6094852
  22.6 20.9 %copy-start.2 = (bf16[1,7,2,128,128]{4,3,2,1,0:T(8,128)(2,1)S(1)}, bf16[1,7,2,128,128]{4,3,2,1,0:T(8,128)(2,1)}, u32[]{:S(2)}) copy-start(bf16[1,7,2,128,128]{4,3,2,1,0:T(8,128)(2,1)} %refs_2_.1) | copy-start | bytes 1376260
  24.4 21.8 %collective-permute-start.1 = (f32[512,128]{1,0:T(8,128)S(1)}, f32[512,128]{1,0:T(8,128)S(1)}, u32[]{:S(2)}, u32[]{:S(2)}) collective-permute-start(f32[512,128]{1,0:T(8,128)S(1)} %get-tuple-element.36), channel_id=1, source_target_pairs={{0,1},{1,0},{2,3},{3,2},{4,5},{5,4},{6,7},{7,6},{8,9},{9,8},{10,11... | collective-permute-start | bytes 786440 | tf_op jit(solution)/shard_map/ppermute | solution.py:466
  25.9 5.1 %collective-permute-start.4 = (f32[64,128]{1,0:T(8,128)S(1)}, f32[64,128]{1,0:T(8,128)S(1)}, u32[]{:S(2)}, u32[]{:S(2)}) collective-permute-start(f32[64,128]{1,0:T(8,128)S(1)} %pair_up.1.own_ref), channel_id=1, source_target_pairs={{0,48},{8,56},{16,32},{24,40},{32,16},{40,24},{48,0},{56,8},{64,11... | collective-permute-start | bytes 98312 | tf_op jit(solution)/shard_map/ppermute | solution.py:466
  29.0 5.4 %collective-permute-start.3 = (f32[64,128]{1,0:T(8,128)S(1)}, f32[64,128]{1,0:T(8,128)S(1)}, u32[]{:S(2)}, u32[]{:S(2)}) collective-permute-start(f32[64,128]{1,0:T(8,128)S(1)} %pair_up.1.own_ref), channel_id=1, source_target_pairs={{0,32},{8,40},{16,48},{24,56},{32,0},{40,8},{48,16},{56,24},{64,96... | collective-permute-start | bytes 98312 | tf_op jit(solution)/shard_map/ppermute | solution.py:466
  29.6 4.8 %collective-permute-start.2 = (f32[64,128]{1,0:T(8,128)S(1)}, f32[64,128]{1,0:T(8,128)S(1)}, u32[]{:S(2)}, u32[]{:S(2)}) collective-permute-start(f32[64,128]{1,0:T(8,128)S(1)} %pair_up.1.own_ref), channel_id=1, source_target_pairs={{0,16},{8,24},{16,0},{24,8},{32,48},{40,56},{48,32},{56,40},{64,80... | collective-permute-start | bytes 98312 | tf_op jit(solution)/shard_map/ppermute | solution.py:466
  35.2 5.1 %collective-permute-start.7 = (f32[64,128]{1,0:T(8,128)S(1)}, f32[64,128]{1,0:T(8,128)S(1)}, u32[]{:S(2)}, u32[]{:S(2)}) collective-permute-start(f32[64,128]{1,0:T(8,128)S(1)} %get-tuple-element.38.top_ref), channel_id=1, source_target_pairs={{0,192},{8,200},{16,208},{24,216},{32,224},{40,232},{48,240},{56,2... | collective-permute-start | bytes 98312 | tf_op jit(solution)/shard_map/ppermute | solution.py:466
  38.0 5.4 %collective-permute-start.6 = (f32[64,128]{1,0:T(8,128)S(1)}, f32[64,128]{1,0:T(8,128)S(1)}, u32[]{:S(2)}, u32[]{:S(2)}) collective-permute-start(f32[64,128]{1,0:T(8,128)S(1)} %get-tuple-element.38.top_ref), channel_id=1, source_target_pairs={{0,128},{8,136},{16,144},{24,152},{32,160},{40,168},{48,176},{56,1... | collective-permute-start | bytes 98312 | tf_op jit(solution)/shard_map/ppermute | solution.py:466
  38.8 4.6 %collective-permute-start.5 = (f32[64,128]{1,0:T(8,128)S(1)}, f32[64,128]{1,0:T(8,128)S(1)}, u32[]{:S(2)}, u32[]{:S(2)}) collective-permute-start(f32[64,128]{1,0:T(8,128)S(1)} %get-tuple-element.38.top_ref), channel_id=1, source_target_pairs={{0,64},{8,72},{16,80},{24,88},{32,96},{40,104},{48,112},{56,120},{... | collective-permute-start | bytes 98312 | tf_op jit(solution)/shard_map/ppermute | solution.py:466
  46.2 19.4 %all-to-all-start.1 = ((f32[8,128,128]{2,1,0:T(8,128)}), f32[8,128,128]{2,1,0:T(8,128)S(1)}, u32[]{:S(2)}, u32[]{:S(2)}) async-start(f32[8,128,128]{2,1,0:T(8,128)} %turn.1), calls=%async_computation.1 | async-start | bytes 1048576 | tf_op jit(solution)/shard_map/all_to_all | solution.py:508
